TPU v7x, 32 devices: a whole 2x2x4 slice. The times are simulated.
32 devices in a mesh: row: 8 (over y, x, core), col: 4 (over z).
Axes of the slice: x: 2, y: 2, z: 4, core: 2. Of those that a mesh axis runs over, the one named last changes fastest.
Arguments:
- velocity: float32 [128, 128, 2048], P(None, 'row', 'col'), may hold values from -6 to 6
- symbol_x: float32 [128], replicated, may hold values from 0.3 to 3
- symbol_y: float32 [128], replicated, may hold values from 0.3 to 3
- symbol_z: float32 [2048], replicated, may hold values from 0.3 to 3
Outputs:
- coefficients: float32 [128, 128, 2048], P('row', 'col')
All inputs are finite; a program needn't handle non-finite values.
Results may differ from a plain program's by a relative error of at most 0.000076.
Values sent between devices are 32-bit elements; how exact they have to be, the bound alone decides.
A program may use at most 192 MiB of HBM per device.

v0:
```python
import jax
import jax.numpy as jnp
from jax import lax
from jax.sharding import PartitionSpec as P


def mode_table(count):
    rank = jnp.arange(count)
    angle = 2.0 * jnp.pi / count * (rank[:, None] * rank[None, :] % count).astype(jnp.float32)
    return (jnp.cos(angle) + jnp.sin(angle)) * count ** (-0.5)


def along_dim(values, dim):
    moved = jnp.tensordot(
        values, mode_table(values.shape[dim]), axes=([dim], [0]), precision=lax.Precision.HIGHEST
    )
    return jnp.moveaxis(moved, -1, dim)


def local(velocity, symbol_x, symbol_y, symbol_z):
    part_values = velocity
    part_values = along_dim(part_values, 0)
    part_values = lax.all_to_all(part_values, "row", split_axis=0, concat_axis=1, tiled=True)
    part_values = along_dim(part_values, 1)
    pencil_values = part_values
    pencil_values = lax.all_to_all(pencil_values, "col", split_axis=1, concat_axis=2, tiled=True)
    pencil_values = along_dim(pencil_values, 2)
    share_x = pencil_values.shape[0]
    part_x = lax.dynamic_slice_in_dim(symbol_x, lax.axis_index("row") * share_x, share_x)
    share_y = pencil_values.shape[1]
    part_y = lax.dynamic_slice_in_dim(symbol_y, lax.axis_index("col") * share_y, share_y)
    symbol = part_x[:, None, None] + part_y[None, :, None] + symbol_z[None, None, :]
    pencil_values = pencil_values * ((1.0 - 0.2 * symbol) / (1.0 + 0.2 * symbol))
    return pencil_values


def solution(mesh):
    placed = (P(None, "row", "col"), P(), P(), P())
    return jax.shard_map(
        local, mesh=mesh, in_specs=placed, out_specs=P("row", "col", None), check_vma=False
    )
```

profile of v0, /device:TPU:0, one launch (start us, length us, event | category | flops | bytes accessed | tf_op | source)
XLA Modules:
  0.0 224.9 jit_solution(18273751174371291723)
XLA Ops:
  0.0 9.0 %fusion.19 = f32[128,16,512]{2,0,1:T(8,128)S(1)} fusion(f32[128,16,512]{2,1,0:T(8,128)} %param.4), kind=kOutput, calls=%fused_computation.20 | convolution fusion | flops 1610874880 | bytes 8388608 | tf_op jit(solution)/shard_map/dot_general | solution.py:14
  9.0 2.4 %copy.24 = f32[128,16,512]{2,1,0:T(8,128)S(1)} copy(f32[128,16,512]{2,0,1:T(8,128)S(1)} %fusion.19) | data formatting | bytes 8388608 | tf_op jit(solution)/shard_map/dot_general | solution.py:14
  11.5 54.0 %all_to_all.36 = f32[128,16,512]{2,1,0:T(8,128)S(1)} all-to-all(f32[128,16,512]{2,1,0:T(8,128)S(1)} %copy.24), channel_id=1, replica_groups=mesh['row'=8,'col'=4] {'row'}, dimensions={0} | all-to-all | bytes 8388608 | tf_op jit(solution)/shard_map/all_to_all | solution.py:23
  65.5 0.8 copy.25
  66.3 8.6 %convolution_bitcast_fusion = f32[16,128,512]{1,2,0:T(8,128)} fusion(f32[16,128,512]{2,1,0:T(8,128)S(1)} %bitcast.28), kind=kOutput, calls=%fused_computation.23 | convolution fusion | flops 1610874880 | bytes 8388608 | tf_op jit(solution)/shard_map/dot_general | solution.py:14
  75.0 5.5 %copy.27 = f32[16,128,512]{2,0,1:T(8,128)} copy(f32[16,128,512]{1,2,0:T(8,128)} %convolution_bitcast_fusion) | data formatting | bytes 8388608 | tf_op jit(solution)/shard_map/transpose | solution.py:17
  80.5 0.0 copy-start.1
  80.5 0.0 copy-start.2
  80.5 5.1 %all-to-all-start.1 = ((f32[16,128,512]{2,0,1:T(8,128)}), f32[16,128,512]{2,0,1:T(8,128)}, u32[]{:S(2)}, u32[]{:S(2)}) async-start(f32[16,128,512]{2,0,1:T(8,128)} %copy.27), calls=%async_computation.1 | async-start | bytes 8388608 | tf_op jit(solution)/shard_map/all_to_all | solution.py:26
  85.6 0.0 copy-done.1
  85.6 0.1 dynamic_slice.7
  85.7 0.0 copy-done.2
  85.7 0.1 dynamic_slice.6
  85.8 0.1 broadcast_add_fusion
  85.9 67.7 %fusion.51 = f32[2048,2048,1]{1,0,2:T(8,128)} fusion(), kind=kLoop, calls=%fused_computation.7.clone.clone.clone.1 | loop fusion | flops 67108864 | bytes 16777216 | tf_op jit(solution)/shard_map/dot_general | solution.py:14
  153.5 25.0 %all-to-all-done.1 = f32[16,128,512]{2,0,1:T(8,128)} async-done(((f32[16,128,512]{2,0,1:T(8,128)}), f32[16,128,512]{2,0,1:T(8,128)}, u32[]{:S(2)}, u32[]{:S(2)}) %all-to-all-start.1) | async-done | bytes 4194336 | tf_op jit(solution)/shard_map/all_to_all | solution.py:26
  178.5 6.9 %copy.29 = f32[16,32,4,512]{3,2,1,0:T(4,128)} copy(f32[16,32,4,512]{3,0,1,2:T(8,128)} %bitcast.8) | data formatting | bytes 8388608 | tf_op jit(solution)/shard_map/all_to_all | solution.py:26
  185.4 0.0 copy-start
  185.4 6.1 %all_to_all.33 = f32[16,32,2048]{2,1,0:T(8,128)} reshape(f32[16,32,4,512]{3,2,1,0:T(4,128)} %copy.29) | data formatting | bytes 8388608 | tf_op jit(solution)/shard_map/all_to_all | solution.py:26
  191.5 0.0 copy-done
  191.5 33.4 %divide_multiply_fusion = f32[16,32,2048]{2,1,0:T(8,128)} fusion(f32[16,32,2048]{2,1,0:T(8,128)} %all_to_all.33, f32[2048]{0:T(1024)S(1)} %copy-done, f32[16,32]{1,0:T(8,128)S(1)} %broadcast_add_fusion, f32[2048,2048,1]{1,0,2:T(8,128)} %fusion.51), kind=kOutput, calls=%fused_computation.22 | convolution fusion | flops 25776095232 | bytes 25176064 | tf_op jit(solution)/shard_map/dot_general | solution.py:14
Async XLA Ops:
  80.5 5.2 %copy-start.1 = (f32[128]{0:T(128)S(1)}, f32[128]{0:T(128)}, u32[]{:S(2)}) copy-start(f32[128]{0:T(128)} %param.6) | copy-start | bytes 1540
  80.5 5.3 %copy-start.2 = (f32[128]{0:T(128)S(1)}, f32[128]{0:T(128)}, u32[]{:S(2)}) copy-start(f32[128]{0:T(128)} %param.5) | copy-start | bytes 1540
  80.5 98.1 %all-to-all-start.1 = ((f32[16,128,512]{2,0,1:T(8,128)}), f32[16,128,512]{2,0,1:T(8,128)}, u32[]{:S(2)}, u32[]{:S(2)}) async-start(f32[16,128,512]{2,0,1:T(8,128)} %copy.27), calls=%async_computation.1 | async-start | bytes 8388608 | tf_op jit(solution)/shard_map/all_to_all | solution.py:26
  185.4 6.1 %copy-start = (f32[2048]{0:T(1024)S(1)}, f32[2048]{0:T(1024)}, u32[]{:S(2)}) copy-start(f32[2048]{0:T(1024)} %param.7) | copy-start | bytes 24580
where the time goes:
time: 225 us
  other arithmetic  67.8 us (30%)
  blocking collectives  54 us (24%)
  matrix products  51 us (23%)
  waiting for transfers between devices  25 us (11%)
  local copies, waits for them, and re-layouts  21.9 us (10%)
  starting transfers between devices  5.15 us (2%)
    dot_general x1, other arithmetic, along_dim(): jnp.tensordot(values, mode_table(values.shape[dim]), axes=([dim], [0]), p...  67.7 us
    all_to_all x1, blocking collectives, local(): lax.all_to_all(part_values, 'row', split_axis=0, concat_axis=1, tiled=True)  54 us
    dot_general x3, matrix products, along_dim(): jnp.tensordot(values, mode_table(values.shape[dim]), axes=([dim], [0]), p...  51 us
    all_to_all x1, waiting for transfers between devices, local(): lax.all_to_all(pencil_values, 'col', split_axis=1, concat_axis=2, tiled=T...  25 us
    all_to_all x2, local copies, waits for them, and re-layouts, local(): lax.all_to_all(pencil_values, 'col', split_axis=1, concat_axis=2, tiled=T...  13 us
    transpose x1, local copies, waits for them, and re-layouts, along_dim(): return jnp.moveaxis(moved, -1, dim)  5.51 us
    all_to_all x1, starting transfers between devices, local(): lax.all_to_all(pencil_values, 'col', split_axis=1, concat_axis=2, tiled=T...  5.15 us
  transfers between devices with their start and end apart: 1, of which 1 were waited for; matrix products, arithmetic and copies ran while one was open for 30% of the time, Pallas kernels for 0%

commit v1 on v0

--- a/solution.py
+++ b/solution.py
@@ -23,7 +23,11 @@
     part_values = lax.all_to_all(part_values, "row", split_axis=0, concat_axis=1, tiled=True)
     part_values = along_dim(part_values, 1)
     pencil_values = part_values
-    pencil_values = lax.all_to_all(pencil_values, "col", split_axis=1, concat_axis=2, tiled=True)
+    teams_divide = lambda sheet: jnp.concatenate(
+        lax.all_to_all(jnp.stack(jnp.split(sheet, lax.axis_size("col"), axis=1)), "col", 0, 0),
+        axis=2,
+    )
+    pencil_values = teams_divide(pencil_values)
     pencil_values = along_dim(pencil_values, 2)
     share_x = pencil_values.shape[0]
     part_x = lax.dynamic_slice_in_dim(symbol_x, lax.axis_index("row") * share_x, share_x)

time: 225 us -> 206 us (0.916)
  local copies, waits for them, and re-layouts: 21.9 us -> 6.86 us
  matrix products: 51 us -> 44.3 us
  other arithmetic: 67.8 us -> 70.3 us
    all_to_all x2 -> x0, local copies, waits for them, and re-layouts: 13 us -> none  [local(): lax.all_to_all(pencil_values, 'col', split_axis=1, concat_axis=2, tiled=T...]
    dot_general x3, matrix products: 51 us -> 44.3 us  [along_dim(): jnp.tensordot(values, mode_table(values.shape[dim]), axes=([dim], [0]), p...]
    transpose x1 -> x0, local copies, waits for them, and re-layouts: 5.51 us -> none  [along_dim(): return jnp.moveaxis(moved, -1, dim)]
    reshape x0 -> x1, local copies, waits for them, and re-layouts: none -> 2.64 us  [local(): jnp.concatenate(lax.all_to_all(jnp.stack(jnp.split(sheet, lax.axis_size('...]
    another operation x0 -> x1, other arithmetic: none -> 2.52 us  [local(): jnp.stack(jnp.split(sheet, lax.axis_size('col'), axis=1))]
  transfers between devices with their start and end apart: 1 -> 1, of which waited for: 1 -> 1; matrix products, arithmetic and copies ran while one was open for 30% -> 33% of each run, Pallas kernels for 0% -> 0%
where the time goes in v1:
time: 206 us
  other arithmetic  70.3 us (34%)
  blocking collectives  54 us (26%)
  matrix products  44.3 us (22%)
  waiting for transfers between devices  25 us (12%)
  local copies, waits for them, and re-layouts  6.86 us (3%)
  starting transfers between devices  5.2 us (3%)
    dot_general x1, other arithmetic, along_dim(): jnp.tensordot(values, mode_table(values.shape[dim]), axes=([dim], [0]), p...  67.7 us
    all_to_all x1, blocking collectives, local(): lax.all_to_all(part_values, 'row', split_axis=0, concat_axis=1, tiled=True)  54 us
    dot_general x3, matrix products, along_dim(): jnp.tensordot(values, mode_table(values.shape[dim]), axes=([dim], [0]), p...  44.3 us
    all_to_all x1, waiting for transfers between devices, local(): lax.all_to_all(jnp.stack(jnp.split(sheet, lax.axis_size('col'), axis=1)),...  25 us
    all_to_all x1, starting transfers between devices, local(): lax.all_to_all(jnp.stack(jnp.split(sheet, lax.axis_size('col'), axis=1)),...  5.2 us
  transfers between devices with their start and end apart: 1, of which 1 were waited for; matrix products, arithmetic and copies ran while one was open for 33% of the time, Pallas kernels for 0%

profile of v1, /device:TPU:0, one launch (start us, length us, event | category | flops | bytes accessed | tf_op | source)
XLA Modules:
  0.0 205.7 jit_solution(4706164993764963773)
XLA Ops:
  0.0 8.4 %fusion.19 = f32[128,16,512]{2,0,1:T(8,128)S(1)} fusion(f32[128,16,512]{2,1,0:T(8,128)} %param.4), kind=kOutput, calls=%fused_computation.21 | convolution fusion | flops 1610874880 | bytes 8388608 | tf_op jit(solution)/shard_map/dot_general | solution.py:14
  8.5 2.4 %copy.11 = f32[128,16,512]{2,1,0:T(8,128)S(1)} copy(f32[128,16,512]{2,0,1:T(8,128)S(1)} %fusion.19) | data formatting | bytes 8388608 | tf_op jit(solution)/shard_map/dot_general | solution.py:14
  10.9 54.0 %all_to_all.23 = f32[128,16,512]{2,1,0:T(8,128)S(1)} all-to-all(f32[128,16,512]{2,1,0:T(8,128)S(1)} %copy.11), channel_id=1, replica_groups=mesh['row'=8,'col'=4] {'row'}, dimensions={0} | all-to-all | bytes 8388608 | tf_op jit(solution)/shard_map/all_to_all | solution.py:23
  64.9 0.8 copy.12
  65.8 4.7 %convolution_bitcast_fusion = f32[16,128,512]{2,1,0:T(8,128)S(1)} fusion(f32[16,128,512]{2,1,0:T(8,128)S(1)} %bitcast.35), kind=kOutput, calls=%fused_computation.24 | convolution fusion | flops 1610874880 | bytes 8388608 | tf_op jit(solution)/shard_map/dot_general | solution.py:14
  70.5 0.8 slice_bitcast_fusion.3
  71.3 2.5 %pad_maximum_fusion = f32[4,16,32,512]{3,2,1,0:T(8,128)} fusion(f32[1,16,32,512]{3,2,1,0:T(8,128)S(1)} %get-tuple-element.6, f32[1,16,32,512]{3,2,1,0:T(8,128)S(1)} %get-tuple-element.7, f32[1,16,32,512]{3,2,1,0:T(8,128)S(1)} %get-tuple-element.8, f32[1,16,32,512]{3,2,1,0:T(8,128)S(1)} %get-tuple-element.5), kind=kLoop, calls=%fused_computation.20 | loop fusion | flops 3145728 | bytes 8388608 | tf_op jit(solution)/shard_map/stack | solution.py:27
  73.8 0.0 copy-start.1
  73.8 0.0 copy-start.2
  73.8 5.2 %all-to-all-start.1 = ((f32[4,16,32,512]{3,2,1,0:T(8,128)}), f32[4,16,32,512]{3,2,1,0:T(8,128)}, u32[]{:S(2)}, u32[]{:S(2)}) async-start(f32[4,16,32,512]{3,2,1,0:T(8,128)} %pad_maximum_fusion), calls=%async_computation.1 | async-start | bytes 8388608 | tf_op jit(solution)/shard_map/all_to_all | solution.py:27
  79.0 0.0 copy-done.1
  79.1 0.1 dynamic_slice.7
  79.1 0.0 copy-done.2
  79.1 0.1 dynamic_slice.6
  79.2 0.1 broadcast_add_fusion
  79.3 67.7 %fusion.51 = f32[2048,2048,1]{1,0,2:T(8,128)} fusion(), kind=kLoop, calls=%fused_computation.7.clone.clone.clone.1 | loop fusion | flops 67108864 | bytes 16777216 | tf_op jit(solution)/shard_map/dot_general | solution.py:14
  147.0 25.0 %all-to-all-done.1 = f32[4,16,32,512]{3,2,1,0:T(8,128)} async-done(((f32[4,16,32,512]{3,2,1,0:T(8,128)}), f32[4,16,32,512]{3,2,1,0:T(8,128)}, u32[]{:S(2)}, u32[]{:S(2)}) %all-to-all-start.1) | async-done | bytes 4194336 | tf_op jit(solution)/shard_map/all_to_all | solution.py:27
  171.9 0.0 copy-start
  171.9 2.6 %copy.14 = f32[4,16,4,8,512]{4,3,0,2,1:T(8,128)S(1)} copy(f32[4,16,4,8,512]{4,3,2,1,0:T(8,128)} %bitcast.12) | data formatting | bytes 8388608 | tf_op jit(solution)/shard_map/reshape | solution.py:26
  174.6 0.0 copy-done
  174.6 31.1 %divide_multiply_fusion = f32[16,32,2048]{2,1,0:T(8,128)} fusion(f32[16,32,2048]{2,1,0:T(8,128)S(1)} %bitcast.36, f32[2048]{0:T(1024)S(1)} %copy-done, f32[16,32]{1,0:T(8,128)S(1)} %broadcast_add_fusion, f32[2048,2048,1]{1,0,2:T(8,128)} %fusion.51), kind=kOutput, calls=%fused_computation.23 | convolution fusion | flops 25776095232 | bytes 25176064 | tf_op jit(solution)/shard_map/dot_general | solution.py:14
Async XLA Ops:
  73.8 5.2 %copy-start.1 = (f32[128]{0:T(128)S(1)}, f32[128]{0:T(128)}, u32[]{:S(2)}) copy-start(f32[128]{0:T(128)} %param.6) | copy-start | bytes 1540
  73.8 5.3 %copy-start.2 = (f32[128]{0:T(128)S(1)}, f32[128]{0:T(128)}, u32[]{:S(2)}) copy-start(f32[128]{0:T(128)} %param.5) | copy-start | bytes 1540
  73.8 98.1 %all-to-all-start.1 = ((f32[4,16,32,512]{3,2,1,0:T(8,128)}), f32[4,16,32,512]{3,2,1,0:T(8,128)}, u32[]{:S(2)}, u32[]{:S(2)}) async-start(f32[4,16,32,512]{3,2,1,0:T(8,128)} %pad_maximum_fusion), calls=%async_computation.1 | async-start | bytes 8388608 | tf_op jit(solution)/shard_map/all_to_all | solution.py:27
  171.9 2.6 %copy-start = (f32[2048]{0:T(1024)S(1)}, f32[2048]{0:T(1024)}, u32[]{:S(2)}) copy-start(f32[2048]{0:T(1024)} %param.7) | copy-start | bytes 24580
